TPU v7x, 512 devices: a whole 4x4x16 slice. The times are simulated.
512 devices in a mesh: dp: 16 (over y_lo, x, core), ctx: 32 (over y_hi, z).
Axes of the slice: x: 4, y: 4 (y_hi: 2, y_lo: 2; y = y_hi * 2 + y_lo), z: 16, core: 2. Of those that a mesh axis runs over, the one named last changes fastest.
Arguments:
- grad_out: bfloat16 [65536, 4096], P(('dp', 'ctx')), may hold values from -24 to 24
- gate: bfloat16 [65536, 4096], P(('dp', 'ctx')), may hold values from -6 to 6
- conv_in: bfloat16 [65536, 4096], P(('dp', 'ctx')), may hold values from -6 to 6
- filt: bfloat16 [4096, 64], P('dp'), may hold values from -0.75 to 0.75
- doc_end: int32 [65536], P(('dp', 'ctx')), may hold values from 1 to 65536, as said below
Outputs:
- grad_in: bfloat16 [65536, 4096], P(('dp', 'ctx'))
- grad_filt: float32 [4096, 64], P('dp')
Inputs may be any that keep to these rules, and one draw needn't show every extreme that they name: doc_end is the same for all rows of one document and larger than the row's own index; no document crosses a multiple of 4096.
All inputs are finite; a program needn't handle non-finite values.
Results may differ from a plain program's by a relative error of at most 0.0049.
Values may be sent and summed in bfloat16 or wider, within the bound.
A program may use at most 64 MiB of HBM per device.

v0:
```python
import jax
import jax.numpy as jnp
from jax import lax
from jax.sharding import PartitionSpec as P


def from_behind(value, axis, steps):
    count = lax.axis_size(axis)
    first, last = (max(0, -steps), min(count, count - steps))
    return lax.ppermute(value, axis, [(source, source + steps) for source in range(first, last)])


def body(grad_out, gate, conv_in, filt, doc_end):
    row_count, channels = grad_out.shape
    tap_count = filt.shape[1]
    group_size = 8
    whole_filter = lax.all_gather(filt, "dp", axis=0, tiled=True)
    filter_rows = whole_filter.T
    grad_y = (grad_out.astype(jnp.float32) * gate.astype(jnp.float32)).astype(jnp.bfloat16)
    following = from_behind(grad_y, "ctx", -1)
    extended = jnp.concatenate([grad_y, following], axis=0)
    first_row = (lax.axis_index("dp") * lax.axis_size("ctx") + lax.axis_index("ctx")) * row_count
    remaining = doc_end - (first_row + jnp.arange(row_count, dtype=jnp.int32))
    within = jnp.arange(group_size, dtype=jnp.int32)

    def one_group(which, state):
        accum, tap_rows = state
        base = (which * group_size).astype(jnp.int32)
        offsets = base + within
        windows = jax.vmap(lambda offset: lax.dynamic_slice_in_dim(extended, offset, row_count, 0))(
            offsets
        )
        inside = (offsets[:, None] < remaining[None, :])[:, :, None]
        windows = jnp.where(inside, windows, jnp.zeros((), jnp.bfloat16))
        weights = lax.dynamic_slice_in_dim(filter_rows, base, group_size, 0)
        accum = accum + jnp.einsum(
            "trc,tc->rc", windows, weights, preferred_element_type=jnp.float32
        )
        tap_block = jnp.einsum("trc,rc->tc", windows, conv_in, preferred_element_type=jnp.float32)
        tap_rows = lax.dynamic_update_slice_in_dim(tap_rows, tap_block, base, 0)
        return (accum, tap_rows)

    start = (
        jnp.zeros((row_count, channels), jnp.float32),
        jnp.zeros((tap_count, channels), jnp.float32),
    )
    accum, tap_rows = lax.fori_loop(0, tap_count // group_size, one_group, start)
    grad_in = accum.astype(jnp.bfloat16)
    filt_terms = tap_rows.T
    owned = lax.psum_scatter(filt_terms, "dp", scatter_dimension=0, tiled=True)
    grad_filt = lax.psum(owned, "ctx")
    return (grad_in, grad_filt)


def solution(mesh):
    placed = (
        P(("dp", "ctx"), None),
        P(("dp", "ctx"), None),
        P(("dp", "ctx"), None),
        P("dp", None),
        P(("dp", "ctx")),
    )
    return jax.shard_map(
        body,
        mesh=mesh,
        in_specs=placed,
        out_specs=(P(("dp", "ctx"), None), P("dp", None)),
        check_vma=False,
    )
```

profile of v0, /device:TPU:6, one launch (start us, length us, event | category | flops | bytes accessed | tf_op | source)
XLA Modules:
  0.0 696.4 jit_solution(7880382249761035540)
XLA Ops:
  11.1 22.0 %all_gather.3 = bf16[4096,64]{0,1:T(8,128)(2,1)} all-gather(bf16[256,64]{0,1:T(8,128)(2,1)} %param.10), channel_id=1, replica_groups=mesh['dp'=16,'ctx'=32] {'dp'}, dimensions={0}, use_global_device_ids=true | all-gather | bytes 557056 | tf_op jit(solution)/shard_map/all_gather | solution.py:17
  39.0 302.4 %while.23 = (s32[]{:T(128)}, f32[128,4096]{1,0:T(8,128)}, f32[64,4096]{1,0:T(8,128)}, bf16[64,4096]{1,0:T(8,128)(2,1)}, s32[128]{0:T(128)S(1)}, /*index=5*/bf16[...) while((s32[]{:T(128)}, f32[128,4096]{1,0:T(8,128)}, ...), condition=%wide.region_1.2_spmd.clone.clone, body=%wide.region_0.1_spmd.clone.sunk.clone | while | flops 34604080 | bytes 66786340 | solution.py:47
  39.9 19.0 %while.22 = (s32[]{:T(128)}, bf16[256,4096]{1,0:T(8,128)(2,1)S(1)}, s32[8,2]{0,1:T(2,128)S(1)}, bf16[8,128,4096]{2,1,0:T(8,128)(2,1)}, s32[]{:T(128)}) while((s32[]{:T(128)}, bf16[256,4096]{1,0:T(8,128)(2,1)S(1)}, s32[8,2]{0,1:T(2,128)S(1)}, bf16[8,128,4096]{2,1,0:T(8,128)(2,1)}, s32[]{:T(128)}) %tuple.56), condition=%wide.while_cond, body=%wide.while_body.sunk | while | flops 2 | bytes 2098265 | solution.py:30
  59.0 8.2 %multiply_reduce_fusion.6 = f32[4096,128]{0,1:T(8,128)} fusion(f32[4096,8]{0,1:T(8,128)S(1)} %bitcast_convert_fusion.6, bf16[8,128,4096]{2,1,0:T(8,128)(2,1)} %get-tuple-element.289, pred[8,128]{1,0:T(8,128)(4,1)S(1)} %broadcast_compare_fusion.3), kind=kLoop, calls=%fused_computation.4.clone.1.clone | loop fusion | flops 16252928 | bytes 10617856 | tf_op jit(solution)/shard_map/while/body/eval_jaxpr/trc,tc->rc/dot_general | solution.py:36
  77.1 19.0 %while.22 = (s32[]{:T(128)}, bf16[256,4096]{1,0:T(8,128)(2,1)S(1)}, s32[8,2]{0,1:T(2,128)S(1)}, bf16[8,128,4096]{2,1,0:T(8,128)(2,1)}, s32[]{:T(128)}) while((s32[]{:T(128)}, bf16[256,4096]{1,0:T(8,128)(2,1)S(1)}, s32[8,2]{0,1:T(2,128)S(1)}, bf16[8,128,4096]{2,1,0:T(8,128)(2,1)}, s32[]{:T(128)}) %tuple.56), condition=%wide.while_cond, body=%wide.while_body.sunk | while | flops 2 | bytes 2098265 | solution.py:30
  96.2 8.2 %multiply_reduce_fusion.6 = f32[4096,128]{0,1:T(8,128)} fusion(f32[4096,8]{0,1:T(8,128)S(1)} %bitcast_convert_fusion.6, bf16[8,128,4096]{2,1,0:T(8,128)(2,1)} %get-tuple-element.289, pred[8,128]{1,0:T(8,128)(4,1)S(1)} %broadcast_compare_fusion.3), kind=kLoop, calls=%fused_computation.4.clone.1.clone | loop fusion | flops 16252928 | bytes 10617856 | tf_op jit(solution)/shard_map/while/body/eval_jaxpr/trc,tc->rc/dot_general | solution.py:36
  104.4 4.0 bitcast_add_fusion.3
  115.0 19.0 %while.22 = (s32[]{:T(128)}, bf16[256,4096]{1,0:T(8,128)(2,1)S(1)}, s32[8,2]{0,1:T(2,128)S(1)}, bf16[8,128,4096]{2,1,0:T(8,128)(2,1)}, s32[]{:T(128)}) while((s32[]{:T(128)}, bf16[256,4096]{1,0:T(8,128)(2,1)S(1)}, s32[8,2]{0,1:T(2,128)S(1)}, bf16[8,128,4096]{2,1,0:T(8,128)(2,1)}, s32[]{:T(128)}) %tuple.56), condition=%wide.while_cond, body=%wide.while_body.sunk | while | flops 2 | bytes 2098265 | solution.py:30
  134.1 8.2 %multiply_reduce_fusion.6 = f32[4096,128]{0,1:T(8,128)} fusion(f32[4096,8]{0,1:T(8,128)S(1)} %bitcast_convert_fusion.6, bf16[8,128,4096]{2,1,0:T(8,128)(2,1)} %get-tuple-element.289, pred[8,128]{1,0:T(8,128)(4,1)S(1)} %broadcast_compare_fusion.3), kind=kLoop, calls=%fused_computation.4.clone.1.clone | loop fusion | flops 16252928 | bytes 10617856 | tf_op jit(solution)/shard_map/while/body/eval_jaxpr/trc,tc->rc/dot_general | solution.py:36
  142.2 4.0 bitcast_add_fusion.3
  152.9 19.0 %while.22 = (s32[]{:T(128)}, bf16[256,4096]{1,0:T(8,128)(2,1)S(1)}, s32[8,2]{0,1:T(2,128)S(1)}, bf16[8,128,4096]{2,1,0:T(8,128)(2,1)}, s32[]{:T(128)}) while((s32[]{:T(128)}, bf16[256,4096]{1,0:T(8,128)(2,1)S(1)}, s32[8,2]{0,1:T(2,128)S(1)}, bf16[8,128,4096]{2,1,0:T(8,128)(2,1)}, s32[]{:T(128)}) %tuple.56), condition=%wide.while_cond, body=%wide.while_body.sunk | while | flops 2 | bytes 2098265 | solution.py:30
  172.0 8.2 %multiply_reduce_fusion.6 = f32[4096,128]{0,1:T(8,128)} fusion(f32[4096,8]{0,1:T(8,128)S(1)} %bitcast_convert_fusion.6, bf16[8,128,4096]{2,1,0:T(8,128)(2,1)} %get-tuple-element.289, pred[8,128]{1,0:T(8,128)(4,1)S(1)} %broadcast_compare_fusion.3), kind=kLoop, calls=%fused_computation.4.clone.1.clone | loop fusion | flops 16252928 | bytes 10617856 | tf_op jit(solution)/shard_map/while/body/eval_jaxpr/trc,tc->rc/dot_general | solution.py:36
  180.1 4.0 bitcast_add_fusion.3
  190.8 19.0 %while.22 = (s32[]{:T(128)}, bf16[256,4096]{1,0:T(8,128)(2,1)S(1)}, s32[8,2]{0,1:T(2,128)S(1)}, bf16[8,128,4096]{2,1,0:T(8,128)(2,1)}, s32[]{:T(128)}) while((s32[]{:T(128)}, bf16[256,4096]{1,0:T(8,128)(2,1)S(1)}, s32[8,2]{0,1:T(2,128)S(1)}, bf16[8,128,4096]{2,1,0:T(8,128)(2,1)}, s32[]{:T(128)}) %tuple.56), condition=%wide.while_cond, body=%wide.while_body.sunk | while | flops 2 | bytes 2098265 | solution.py:30
  209.8 8.2 %multiply_reduce_fusion.6 = f32[4096,128]{0,1:T(8,128)} fusion(f32[4096,8]{0,1:T(8,128)S(1)} %bitcast_convert_fusion.6, bf16[8,128,4096]{2,1,0:T(8,128)(2,1)} %get-tuple-element.289, pred[8,128]{1,0:T(8,128)(4,1)S(1)} %broadcast_compare_fusion.3), kind=kLoop, calls=%fused_computation.4.clone.1.clone | loop fusion | flops 16252928 | bytes 10617856 | tf_op jit(solution)/shard_map/while/body/eval_jaxpr/trc,tc->rc/dot_general | solution.py:36
  218.0 4.0 bitcast_add_fusion.3
  228.7 19.0 %while.22 = (s32[]{:T(128)}, bf16[256,4096]{1,0:T(8,128)(2,1)S(1)}, s32[8,2]{0,1:T(2,128)S(1)}, bf16[8,128,4096]{2,1,0:T(8,128)(2,1)}, s32[]{:T(128)}) while((s32[]{:T(128)}, bf16[256,4096]{1,0:T(8,128)(2,1)S(1)}, s32[8,2]{0,1:T(2,128)S(1)}, bf16[8,128,4096]{2,1,0:T(8,128)(2,1)}, s32[]{:T(128)}) %tuple.56), condition=%wide.while_cond, body=%wide.while_body.sunk | while | flops 2 | bytes 2098265 | solution.py:30
  247.7 8.2 %multiply_reduce_fusion.6 = f32[4096,128]{0,1:T(8,128)} fusion(f32[4096,8]{0,1:T(8,128)S(1)} %bitcast_convert_fusion.6, bf16[8,128,4096]{2,1,0:T(8,128)(2,1)} %get-tuple-element.289, pred[8,128]{1,0:T(8,128)(4,1)S(1)} %broadcast_compare_fusion.3), kind=kLoop, calls=%fused_computation.4.clone.1.clone | loop fusion | flops 16252928 | bytes 10617856 | tf_op jit(solution)/shard_map/while/body/eval_jaxpr/trc,tc->rc/dot_general | solution.py:36
  266.5 19.0 %while.22 = (s32[]{:T(128)}, bf16[256,4096]{1,0:T(8,128)(2,1)S(1)}, s32[8,2]{0,1:T(2,128)S(1)}, bf16[8,128,4096]{2,1,0:T(8,128)(2,1)}, s32[]{:T(128)}) while((s32[]{:T(128)}, bf16[256,4096]{1,0:T(8,128)(2,1)S(1)}, s32[8,2]{0,1:T(2,128)S(1)}, bf16[8,128,4096]{2,1,0:T(8,128)(2,1)}, s32[]{:T(128)}) %tuple.56), condition=%wide.while_cond, body=%wide.while_body.sunk | while | flops 2 | bytes 2098265 | solution.py:30
  285.6 8.2 %multiply_reduce_fusion.6 = f32[4096,128]{0,1:T(8,128)} fusion(f32[4096,8]{0,1:T(8,128)S(1)} %bitcast_convert_fusion.6, bf16[8,128,4096]{2,1,0:T(8,128)(2,1)} %get-tuple-element.289, pred[8,128]{1,0:T(8,128)(4,1)S(1)} %broadcast_compare_fusion.3), kind=kLoop, calls=%fused_computation.4.clone.1.clone | loop fusion | flops 16252928 | bytes 10617856 | tf_op jit(solution)/shard_map/while/body/eval_jaxpr/trc,tc->rc/dot_general | solution.py:36
  304.4 19.0 %while.22 = (s32[]{:T(128)}, bf16[256,4096]{1,0:T(8,128)(2,1)S(1)}, s32[8,2]{0,1:T(2,128)S(1)}, bf16[8,128,4096]{2,1,0:T(8,128)(2,1)}, s32[]{:T(128)}) while((s32[]{:T(128)}, bf16[256,4096]{1,0:T(8,128)(2,1)S(1)}, s32[8,2]{0,1:T(2,128)S(1)}, bf16[8,128,4096]{2,1,0:T(8,128)(2,1)}, s32[]{:T(128)}) %tuple.56), condition=%wide.while_cond, body=%wide.while_body.sunk | while | flops 2 | bytes 2098265 | solution.py:30
  323.5 8.2 %multiply_reduce_fusion.6 = f32[4096,128]{0,1:T(8,128)} fusion(f32[4096,8]{0,1:T(8,128)S(1)} %bitcast_convert_fusion.6, bf16[8,128,4096]{2,1,0:T(8,128)(2,1)} %get-tuple-element.289, pred[8,128]{1,0:T(8,128)(4,1)S(1)} %broadcast_compare_fusion.3), kind=kLoop, calls=%fused_computation.4.clone.1.clone | loop fusion | flops 16252928 | bytes 10617856 | tf_op jit(solution)/shard_map/while/body/eval_jaxpr/trc,tc->rc/dot_general | solution.py:36
  341.5 70.3 %reduce-scatter.2.cloned.1.call-done = f32[256,64]{0,1:T(8,128)} async-done(((f32[4096,64]{0,1:T(8,128)}), f32[256,64]{0,1:T(8,128)}) %reduce-scatter.2.cloned.1.call-update) | async-done | bytes 65552 | tf_op jit(solution)/shard_map/reduce_scatter | solution.py:50
  414.4 273.7 %all-reduce.3.cloned.1.call-done = f32[256,64]{0,1:T(8,128)} async-done(((f32[256,64]{0,1:T(8,128)}), f32[256,64]{0,1:T(8,128)}) %all-reduce.3.cloned.1.call-update) | async-done | bytes 65552 | tf_op jit(solution)/shard_map/psum | solution.py:51
  (301 shorter events, 234.5 us)
Async XLA Ops:
  7.2 31.8 %copy-start.1 = (bf16[128,4096]{1,0:T(8,128)(2,1)S(1)}, bf16[128,4096]{1,0:T(8,128)(2,1)}, u32[]{:S(2)}) copy-start(bf16[128,4096]{1,0:T(8,128)(2,1)} %param.9) | copy-start | bytes 3145732
  7.2 404.6 %reduce-scatter.2.cloned.1.call-start = ((), (), s32[]{:S(2)}) async-start(), calls=%async_computation.1 | async-start | bytes 1114112 | tf_op jit(solution)/shard_map/reduce_scatter | solution.py:50
  9.1 24.0 %copy-start.2 = (bf16[128,4096]{1,0:T(8,128)(2,1)}, bf16[128,4096]{1,0:T(8,128)(2,1)S(1)}, u32[]{:S(2)}) copy-start(bf16[128,4096]{1,0:T(8,128)(2,1)S(1)} %multiply_convert_fusion) | copy-start | bytes 3145732
  9.1 27.1 %collective-permute-start = (bf16[128,4096]{1,0:T(8,128)(2,1)S(1)}, bf16[128,4096]{1,0:T(8,128)(2,1)}, u32[]{:S(2)}, u32[]{:S(2)}) collective-permute-start(bf16[128,4096]{1,0:T(8,128)(2,1)S(1)} %multiply_convert_fusion), channel_id=1, source_target_pairs={{1,0},{2,1},{3,2},{4,3},{5,4},{6,5},{7,6},{8,7},{9,8},{10,9},{11,1... | collective-permute-start | bytes 3145736 | tf_op jit(solution)/shard_map/ppermute | solution.py:10
  67.1 4.8 copy-start
  104.4 5.4 copy-start
  142.2 5.4 copy-start
  180.1 5.4 copy-start
  218.0 5.4 copy-start
  255.9 5.4 copy-start
  293.7 5.4 copy-start
  331.6 5.4 copy-start
  341.4 346.7 %all-reduce.3.cloned.1.call-start = ((), (), s32[]{:S(2)}) async-start(), calls=%async_computation.2 | async-start | bytes 131072 | tf_op jit(solution)/shard_map/psum | solution.py:51
Sparse Core Ops, SparseCore 0:
  341.6 70.1 reduce-scatter.1
  414.6 273.4 all-reduce.2
where the time goes:
time: 698 us; the launch traced here: 696 us
  waiting for transfers between devices  347 us (50%)
  local copies, waits for them, and re-layouts  169 us (24%)
  other arithmetic  142 us (20%)
  blocking collectives  22 us (3%)
  between operations  14.1 us (2%)
    psum x1, waiting for transfers between devices, body(): grad_filt = lax.psum(owned, 'ctx')  274 us
    gather x192, local copies, waits for them, and re-layouts  152 us
    reduce_scatter x1, waiting for transfers between devices, body(): owned = lax.psum_scatter(filt_terms, 'dp', scatter_dimension=0, tiled=True)  70.3 us
    dot_general x8, other arithmetic, one_group(): jnp.einsum('trc,tc->rc', windows, weights, preferred_element_type=jnp.flo...  65.2 us
    add x8, other arithmetic, one_group(): accum + jnp.einsum('trc,tc->rc', windows, weights, preferred_element_type...  31.5 us
    dot_general x8, other arithmetic, one_group(): jnp.einsum('trc,rc->tc', windows, conv_in, preferred_element_type=jnp.flo...  29.6 us
    all_gather x1, blocking collectives, body(): whole_filter = lax.all_gather(filt, 'dp', axis=0, tiled=True)  22 us
  transfers between devices with their start and end apart: 3, of which 3 were waited for; matrix products, arithmetic and copies ran while one was open for 0% of the time, Pallas kernels for 0%

commit v1 on v0

v1 whole, which is shorter than its diff:
```python
import functools

import jax
import jax.numpy as jnp
from jax import lax
from jax.experimental import pallas as pl
from jax.experimental.pallas import tpu as pltpu
from jax.sharding import PartitionSpec as P

F32 = jnp.float32
BF16 = jnp.bfloat16
LANES = 128
SUB = 16
ROWS = 32
MESH = pl.DeviceIdType.MESH


def kernel(nz, doc_end, grad_out, gate, conv_in, taps_own, grad_in, grad_filt,
           go_v, gate_v, x_v, gy_v, halo_v, g_s, x_s, f_s, stage, limits, terms, taps_all, send, recv, zbuf, ybuf,
           o32, obuf, in_sem, halo_send, halo_recv, tap_send, tap_recv, rs_send, rs_recv,
           z_send, z_recv, y_send, y_recv, out_sem):
    rows, channels = go_v.shape
    half = gy_v.shape[1]
    taps = 2 * half
    tiles = channels // LANES
    owners = taps_all.shape[0]
    group = 2 * owners

    d = lax.axis_index("dp")
    c = lax.axis_index("ctx")
    yh = c // nz
    z = c % nz
    me = d * 2 + yh
    first_row = (d * (2 * nz) + c) * rows

    def plane_peer(q):
        return {"dp": q // 2, "ctx": (q % 2) * nz + z}

    def depth_peer(other):
        return {"ctx": yh * nz + other}

    before = {"ctx": (c + 2 * nz - 1) % (2 * nz)}
    after = {"ctx": (c + 1) % (2 * nz)}

    barrier = pltpu.get_barrier_semaphore()

    def greet_plane(k, carry):
        pl.semaphore_signal(barrier, inc=1, device_id=plane_peer((me + k) % group), device_id_type=MESH)
        return carry

    def greet_depth(k, carry):
        pl.semaphore_signal(barrier, inc=1, device_id=depth_peer((z + k) % nz), device_id_type=MESH)
        return carry

    pl.semaphore_signal(barrier, inc=1, device_id=before, device_id_type=MESH)
    pl.semaphore_signal(barrier, inc=1, device_id=after, device_id_type=MESH)
    lax.fori_loop(1, nz, greet_depth, 0)
    lax.fori_loop(1, group, greet_plane, 0)

    loads = []
    for part in range(2):
        rng = pl.ds(part * half * 2, half * 2)
        for which, (src, dst) in enumerate(((grad_out, go_v), (gate, gate_v), (conv_in, x_v))):
            loads.append(pltpu.make_async_copy(src.at[rng], dst.at[rng], in_sem.at[part * 3 + which]))
            loads[-1].start()

    def place(block, h, tile):
        at = (tile // SUB) * (16 * SUB) + h * 8 * SUB + tile % SUB
        stage[pl.ds(at, 8, stride=SUB), :] = block

    def settle(dst, base):
        at = pl.ds(pl.multiple_of(base * SUB, 16 * SUB), 16 * SUB)
        for side in range(2):
            dst[at, side * LANES:(side + 1) * LANES] = (
                stage[side * 16 * SUB:(side + 1) * 16 * SUB, :].astype(BF16))

    def spread(dst, base, blocks):
        for j, block in enumerate(blocks):
            for h in range(2):
                place(block[h * 8:(h + 1) * 8], h, j)
        settle(dst, base)

    def spread_inputs(a, carry, to_send):
        at = pl.multiple_of(a * 16, 16)
        blocks = []
        for j in range(tiles):
            cols = slice(j * LANES, (j + 1) * LANES)
            y = go_v[pl.ds(at, 16), cols].astype(F32) * gate_v[pl.ds(at, 16), cols].astype(F32)
            y = y.astype(BF16)
            if to_send:
                gy_v[a // 2, pl.ds(pl.multiple_of((a % 2) * 16, 16), 16), cols] = y
            blocks.append(y.astype(F32))
        spread(g_s, at, blocks)
        spread(x_s, at, [x_v[pl.ds(at, 16), j * LANES:(j + 1) * LANES].astype(F32) for j in range(tiles)])
        return carry

    width = 16 * SUB
    term = lax.broadcasted_iota(jnp.int32, (SUB, width), 1)
    kept = jnp.where(term % SUB == lax.broadcasted_iota(jnp.int32, (SUB, width), 0), 1.0, 0.0)
    place_of = (term // SUB).astype(F32)

    def reach(i):
        return (doc_end[i] - (first_row + i)).astype(F32)

    def fill_limits(ib, carry):
        v = jnp.zeros((SUB, width), F32)
        for r in range(16):
            v = jnp.where(term // SUB == r, reach(ib * 16 + r), v)
        limits[pl.ds(pl.multiple_of(ib * SUB, SUB), SUB), :] = v
        return carry

    lax.fori_loop(0, rows // 16, fill_limits, 0)

    for copy in loads[:3]:
        copy.wait()
    lax.fori_loop(0, rows // 32, functools.partial(spread_inputs, to_send=True), 0)
    for copy in loads[3:]:
        copy.wait()
    lax.fori_loop(rows // 32, rows // 16, functools.partial(spread_inputs, to_send=False), 0)

    pl.semaphore_wait(barrier, group - 1 + nz - 1 + 2)

    halos = []
    for part in range(2):
        halos.append(pltpu.make_async_remote_copy(
            src_ref=gy_v.at[part], dst_ref=halo_v.at[part], send_sem=halo_send.at[part],
            recv_sem=halo_recv.at[part], device_id=before, device_id_type=MESH))
        halos[-1].start()

    def tap_copy(peer, slot):
        return pltpu.make_async_remote_copy(
            src_ref=taps_own, dst_ref=taps_all.at[slot], send_sem=tap_send.at[peer],
            recv_sem=tap_recv.at[slot], device_id={"dp": peer}, device_id_type=MESH)

    def send_taps(k, carry):
        tap_copy((d + k) % owners, d).start()
        return carry

    lax.fori_loop(1, owners, send_taps, 0)
    taps_all[d] = taps_own[...]

    def tile_of(ref, index):
        return ref[pl.ds(pl.multiple_of(index * SUB, SUB), width), :]

    def add_to(ref, index, value):
        count = ref.shape[0] // (2 * SUB)
        for side in range(2):
            at = pl.ds(pl.multiple_of((side * count + index) * SUB, SUB), SUB)
            ref[at, :] = ref[at, :] + value[:, side * LANES:(side + 1) * LANES]

    def masked(inside):
        return jnp.where(inside, kept, 0.0).astype(BF16)

    def clear(ref):
        def one(k, carry):
            ref[pl.ds(pl.multiple_of(k * 32, 32), 32), :] = jnp.zeros((32, LANES), F32)
            return carry

        lax.fori_loop(0, ref.shape[0] // 32, one, 0)

    def filter_terms(low, high, part):
        def sixteen(ib, carry):
            xt = tile_of(x_s, ib * 16)
            limit = limits[pl.ds(pl.multiple_of(ib * SUB, SUB), SUB), :]
            for u in range(half):
                t = part * half + u
                product = tile_of(g_s, ib * 16 + t) * xt
                add_to(terms, t, jnp.dot(masked(limit > t), product, preferred_element_type=F32))
            return carry

        lax.fori_loop(low, high, sixteen, 0)

    def plane_copy(q, slot):
        return pltpu.make_async_remote_copy(
            src_ref=send.at[q], dst_ref=recv.at[slot], send_sem=rs_send.at[q],
            recv_sem=rs_recv.at[slot], device_id=plane_peer(q), device_id_type=MESH)

    def out_copy(a):
        rng = pl.ds(pl.multiple_of(a * 16, 16), 16)
        return pltpu.make_async_copy(obuf.at[rng], grad_in.at[rng], out_sem.at[a])

    def input_rows(chunk, carry):
        clear(o32)

        def sixteen_taps(tb, carry):
            ft = tile_of(f_s, tb * 16)
            tap = place_of + (tb * 16).astype(F32)
            for u in range(ROWS):
                i = chunk * ROWS + u
                product = tile_of(g_s, i + tb * 16) * ft
                add_to(o32, u, jnp.dot(masked(tap < reach(i)), product, preferred_element_type=F32))
            return carry

        lax.fori_loop(0, taps // 16, sixteen_taps, 0)
        for a in range(ROWS // 16):
            at = pl.multiple_of(chunk * ROWS + a * 16, 16)
            for j in range(tiles):
                base = ((j // SUB) * ROWS + a * 16) * SUB + j % SUB
                v = [o32[pl.ds(base + h * 8 * SUB, 8, stride=SUB), :] for h in range(2)]
                obuf[pl.ds(at, 16), j * LANES:(j + 1) * LANES] = jnp.concatenate(v, axis=0).astype(BF16)
        return carry

    clear(terms)
    cut = rows // 16 - half // 16
    filter_terms(0, cut, 0)
    filter_terms(0, cut - half // 16, 1)

    for part in range(2):
        halos[part].wait_recv()

        def spread_halo(a, carry):
            at = pl.multiple_of(a * 16, 16)
            spread(g_s, rows + part * half + at,
                   [halo_v[part, pl.ds(at, 16), j * LANES:(j + 1) * LANES].astype(F32) for j in range(tiles)])
            return carry

        lax.fori_loop(0, half // 16, spread_halo, 0)
        filter_terms(cut - part * (half // 16), rows // 16, part)

        def pack(p, carry):
            for jj in range(2):
                tile = p * 2 + jj
                for tg in range(half // 16):
                    base = ((tile // SUB) * taps + part * half + tg * 16) * SUB + tile % SUB
                    v = [terms[pl.ds(base + h * 8 * SUB, 8, stride=SUB), :] for h in range(2)]
                    send[p * 2 + part, tg * 16:(tg + 1) * 16, jj * LANES:(jj + 1) * LANES] = (
                        jnp.concatenate(v, axis=0).astype(BF16))
            return carry

        lax.fori_loop(0, owners, pack, 0)

        def send_terms(k, carry):
            q = ((d + k) % owners) * 2 + part

            @pl.when(q != me)
            def _():
                plane_copy(q, me).start()

            return carry

        lax.fori_loop(0, owners, send_terms, 0)

        if part == 0:
            def take_taps(k, carry):
                p = (d + k) % owners
                tap_copy(p, p).wait_recv()
                return carry

            lax.fori_loop(1, owners, take_taps, 0)

            def spread_taps(a, carry):
                at = pl.multiple_of(a * 16, 16)
                spread(f_s, at, [taps_all[j // 2, pl.ds(at, 16), (j % 2) * LANES:(j % 2 + 1) * LANES].astype(F32)
                                 for j in range(tiles)])
                return carry

            lax.fori_loop(0, taps // 16, spread_taps, 0)
            input_rows(0, 0)

    recv[me] = send[me]
    lax.fori_loop(1, 3, input_rows, 0)

    def take_terms(k, carry):
        s = (me + k) % group
        plane_copy(s, s).wait_recv()
        return carry

    lax.fori_loop(1, group, take_terms, 0)
    zero_half = jnp.zeros((half, recv.shape[2]), F32)
    summed = lax.fori_loop(0, group, lambda s, acc: acc + recv[s].astype(F32), zero_half)
    zbuf[z] = summed.astype(BF16)

    def depth_copy(other, slot):
        return pltpu.make_async_remote_copy(
            src_ref=zbuf.at[z], dst_ref=zbuf.at[slot], send_sem=z_send.at[other],
            recv_sem=z_recv.at[slot], device_id=depth_peer(other), device_id_type=MESH)

    def send_depth(k, carry):
        depth_copy((z + k) % nz, z).start()
        return carry

    lax.fori_loop(1, nz, send_depth, 0)
    lax.fori_loop(3, rows // ROWS, input_rows, 0)

    def take_depth(k, carry):
        other = (z + k) % nz
        depth_copy(other, other).wait_recv()
        return carry

    lax.fori_loop(1, nz, take_depth, 0)
    ybuf[yh] = lax.fori_loop(0, nz, lambda s, acc: acc + zbuf[s].astype(F32), zero_half)

    def swap_copy(slot):
        return pltpu.make_async_remote_copy(
            src_ref=ybuf.at[yh], dst_ref=ybuf.at[slot], send_sem=y_send, recv_sem=y_recv,
            device_id={"ctx": (1 - yh) * nz + z}, device_id_type=MESH)

    swap_copy(yh).start()

    def start_out(a, carry):
        out_copy(a).start()
        return carry

    lax.fori_loop(0, rows // 16, start_out, 0)
    swap_copy(1 - yh).wait_recv()
    grad_filt[0:half, :] = ybuf[0]
    grad_filt[half:taps, :] = ybuf[1]

    def end_out(a, carry):
        out_copy(a).wait()
        return carry

    lax.fori_loop(0, rows // 16, end_out, 0)
    for copy in halos:
        copy.wait_send()
    swap_copy(yh).wait_send()

    def end_taps(k, carry):
        tap_copy((d + k) % owners, d).wait_send()
        return carry

    def end_terms(k, carry):
        plane_copy((me + k) % group, me).wait_send()
        return carry

    def end_depth(k, carry):
        depth_copy((z + k) % nz, z).wait_send()
        return carry

    lax.fori_loop(1, owners, end_taps, 0)
    lax.fori_loop(1, group, end_terms, 0)
    lax.fori_loop(1, nz, end_depth, 0)


def body(grad_out, gate, conv_in, filt, doc_end):
    rows, channels = grad_out.shape
    owned, taps = filt.shape
    half = taps // 2
    owners = lax.axis_size("dp")
    nz = lax.axis_size("ctx") // 2
    group = 2 * owners
    any_space = pl.BlockSpec(memory_space=pl.ANY)
    vmem = pl.BlockSpec(memory_space=pltpu.VMEM)
    dma = pltpu.SemaphoreType.DMA
    grad_in, grad_filt = pl.pallas_call(
        functools.partial(kernel, nz),
        out_shape=(
            jax.ShapeDtypeStruct((rows, channels), BF16),
            jax.ShapeDtypeStruct((taps, owned), F32),
        ),
        in_specs=[pl.BlockSpec(memory_space=pltpu.SMEM), any_space, any_space, any_space, vmem],
        out_specs=(any_space, vmem),
        scratch_shapes=[
            pltpu.VMEM((rows, channels), BF16),
            pltpu.VMEM((rows, channels), BF16),
            pltpu.VMEM((rows, channels), BF16),
            pltpu.VMEM((2, half, channels), BF16),
            pltpu.VMEM((2, half, channels), BF16),
            pltpu.VMEM(((rows + taps) * SUB, 2 * LANES), BF16),
            pltpu.VMEM((rows * SUB, 2 * LANES), BF16),
            pltpu.VMEM((taps * SUB, 2 * LANES), BF16),
            pltpu.VMEM((2 * 16 * SUB, LANES), F32),
            pltpu.VMEM((rows, 16 * SUB), F32),
            pltpu.VMEM((2 * taps * SUB, LANES), F32),
            pltpu.VMEM((owners, taps, owned), BF16),
            pltpu.VMEM((group, half, owned), BF16),
            pltpu.VMEM((group, half, owned), BF16),
            pltpu.VMEM((nz, half, owned), BF16),
            pltpu.VMEM((2, half, owned), F32),
            pltpu.VMEM((2 * ROWS * SUB, LANES), F32),
            pltpu.VMEM((rows, channels), BF16),
            dma((6,)),
            dma((2,)),
            dma((2,)),
            dma((owners,)),
            dma((owners,)),
            dma((group,)),
            dma((group,)),
            dma((nz,)),
            dma((nz,)),
            dma,
            dma,
            dma((rows // 16,)),
        ],
        compiler_params=pltpu.CompilerParams(collective_id=0, has_side_effects=True),
        name="conv_backward",
    )(doc_end, grad_out, gate, conv_in, filt.T)
    return grad_in, grad_filt.T


def solution(mesh):
    placed = (
        P(("dp", "ctx"), None),
        P(("dp", "ctx"), None),
        P(("dp", "ctx"), None),
        P("dp", None),
        P(("dp", "ctx")),
    )
    return jax.shard_map(
        body,
        mesh=mesh,
        in_specs=placed,
        out_specs=(P(("dp", "ctx"), None), P("dp", None)),
        check_vma=False,
    )
```

time: 698 us -> 66.9 us (0.10)
  the two profiles are of different devices: /device:TPU:6 before, /device:TPU:32 now
where the time goes in v1:
time: 66.9 us; the launch traced here: 66.7 us
  Pallas kernels  63.1 us (94%)
  local copies, waits for them, and re-layouts  2.95 us (4%)
    pallas_call x1, Pallas kernels, body(): pl.pallas_call(functools.partial(kernel, nz), out_shape=(jax.ShapeDtypeSt...  63.1 us
    unnamed x4, local copies, waits for them, and re-layouts  2.95 us

profile of v1, /device:TPU:32, one launch (start us, length us, event | category | flops | bytes accessed | tf_op | source)
XLA Modules:
  0.0 66.7 jit_solution(4777258993283631787)
XLA Ops:
  0.6 63.1 %conv_backward.1 = (bf16[128,4096]{1,0:T(8,128)(2,1)}, f32[64,256]{1,0:T(8,128)}) custom-call(s32[128]{0:T(128)} %doc_end.1, bf16[128,4096]{1,0:T(8,128)(2,1)} %grad_out.1, bf16[128,4096]{1,0:T(8,128)(2,1)} %gate.1, bf16[128,4096]{1,0:T(8,128)(2,1)} %conv_in.1, bf16[64,256]{1,0:T(8,128)(2,1)} %bitcast.3), custom_call_target="tpu_custom_call" | custom-call | tf_op jit(solution)/shard_map/conv_backward/pallas_call | solution.py:345
  63.7 0.0 copy-start
  63.7 2.3 %copy.9 = bf16[128,4096]{1,0:T(8,128)(2,1)} copy(bf16[128,4096]{1,0:T(8,128)(2,1)} %get-tuple-element.8) | data formatting | bytes 2097152
  66.0 0.0 copy-done
  66.0 0.6 copy.10
Async XLA Ops:
  63.7 2.3 %copy-start = (f32[64,256]{1,0:T(8,128)S(1)}, f32[64,256]{1,0:T(8,128)}, u32[]{:S(2)}) copy-start(f32[64,256]{1,0:T(8,128)} %get-tuple-element.5) | copy-start | bytes 196612

commit v2 on v1

--- a/solution.py
+++ b/solution.py
@@ -16,31 +16,41 @@
 
 
 def kernel(nz, doc_end, grad_out, gate, conv_in, taps_own, grad_in, grad_filt,
-           go_v, gate_v, x_v, gy_v, halo_v, g_s, x_s, f_s, stage, limits, terms, taps_all, send, recv, zbuf, ybuf,
-           o32, obuf, in_sem, halo_send, halo_recv, tap_send, tap_recv, rs_send, rs_recv,
+           go_v, gate_v, x_v, gy_v, halo_v, g_s, x_s, f_s, stage, limits, terms, taps_all, send, pair, recv, zbuf, ybuf,
+           o32, obuf, in_sem, halo_send, halo_recv, hand_send, hand_recv, tap_send, tap_recv, share_send,
+           pair_send, pair_recv, rs_send, rs_recv,
            z_send, z_recv, y_send, y_recv, out_sem):
     rows, channels = go_v.shape
     half = gy_v.shape[1]
     taps = 2 * half
     tiles = channels // LANES
     owners = taps_all.shape[0]
-    group = 2 * owners
+    group = owners
+    chips = owners // 2
 
     d = lax.axis_index("dp")
     c = lax.axis_index("ctx")
     yh = c // nz
     z = c % nz
-    me = d * 2 + yh
+    core = d % 2
+    me = (d // 2) * 2 + yh
     first_row = (d * (2 * nz) + c) * rows
 
     def plane_peer(q):
-        return {"dp": q // 2, "ctx": (q % 2) * nz + z}
+        return {"dp": (q // 2) * 2 + core, "ctx": (q % 2) * nz + z}
+
+    twin = {"dp": (d // 2) * 2 + 1 - core}
 
     def depth_peer(other):
         return {"ctx": yh * nz + other}
 
-    before = {"ctx": (c + 2 * nz - 1) % (2 * nz)}
-    after = {"ctx": (c + 1) % (2 * nz)}
+    last = 2 * nz - 1
+    members = lax.axis_size("dp")
+    across = (d + members // 2) % members
+    hands_on = c == nz - 1
+    before = {"dp": jnp.where(c == nz, across, d), "ctx": (c + last) % (last + 1)}
+    after = {"dp": jnp.where(hands_on, across, d), "ctx": (c + 1) % (last + 1)}
+    slot = jnp.where(hands_on, 1, 0)
 
     barrier = pltpu.get_barrier_semaphore()
 
@@ -49,12 +59,19 @@
         return carry
 
     def greet_depth(k, carry):
-        pl.semaphore_signal(barrier, inc=1, device_id=depth_peer((z + k) % nz), device_id_type=MESH)
-        return carry
-
+        far = nz // 2 - k
+        pl.semaphore_signal(barrier, inc=1, device_id=depth_peer((z + far) % nz), device_id_type=MESH)
+
+        @pl.when(k > 0)
+        def _():
+            pl.semaphore_signal(barrier, inc=1, device_id=depth_peer((z + nz - far) % nz), device_id_type=MESH)
+
+        return carry
+
+    lax.fori_loop(0, nz // 2, greet_depth, 0)
     pl.semaphore_signal(barrier, inc=1, device_id=before, device_id_type=MESH)
     pl.semaphore_signal(barrier, inc=1, device_id=after, device_id_type=MESH)
-    lax.fori_loop(1, nz, greet_depth, 0)
+    pl.semaphore_signal(barrier, inc=1, device_id=twin, device_id_type=MESH)
     lax.fori_loop(1, group, greet_plane, 0)
 
     loads = []
@@ -109,8 +126,6 @@
         limits[pl.ds(pl.multiple_of(ib * SUB, SUB), SUB), :] = v
         return carry
 
-    lax.fori_loop(0, rows // 16, fill_limits, 0)
-
     for copy in loads[:3]:
         copy.wait()
     lax.fori_loop(0, rows // 32, functools.partial(spread_inputs, to_send=True), 0)
@@ -118,25 +133,82 @@
         copy.wait()
     lax.fori_loop(rows // 32, rows // 16, functools.partial(spread_inputs, to_send=False), 0)
 
-    pl.semaphore_wait(barrier, group - 1 + nz - 1 + 2)
-
-    halos = []
-    for part in range(2):
-        halos.append(pltpu.make_async_remote_copy(
-            src_ref=gy_v.at[part], dst_ref=halo_v.at[part], send_sem=halo_send.at[part],
-            recv_sem=halo_recv.at[part], device_id=before, device_id_type=MESH))
-        halos[-1].start()
-
-    def tap_copy(peer, slot):
-        return pltpu.make_async_remote_copy(
-            src_ref=taps_own, dst_ref=taps_all.at[slot], send_sem=tap_send.at[peer],
-            recv_sem=tap_recv.at[slot], device_id={"dp": peer}, device_id_type=MESH)
+    pl.semaphore_wait(barrier, group - 1 + 1 + nz - 1 + 2)
+
+    pieces = taps // 8
+
+    def piece(ref, k):
+        return ref.at[k // (half // 8), pl.ds((k % (half // 8)) * 8, 8)]
+
+    def halo_copy(k):
+        return pltpu.make_async_remote_copy(
+            src_ref=piece(gy_v, k), dst_ref=piece(halo_v.at[0], k), send_sem=halo_send.at[k],
+            recv_sem=halo_recv.at[k], device_id=before, device_id_type=MESH)
+
+    def hand_copy(k):
+        return pltpu.make_async_remote_copy(
+            src_ref=piece(halo_v.at[0], k), dst_ref=piece(halo_v.at[1], k), send_sem=hand_send.at[k],
+            recv_sem=hand_recv.at[k], device_id={"dp": across}, device_id_type=MESH)
+
+    def hand_on(low, high):
+        @pl.when(hands_on)
+        def _():
+            for k in range(low, high):
+                halo_copy(k).wait_recv()
+                hand_copy(k).start()
+
+    def take_halo(part):
+        low, high = part * pieces // 2, (part + 1) * pieces // 2
+
+        @pl.when(hands_on)
+        def _():
+            for k in range(low, high):
+                hand_copy(k).wait_recv()
+
+        @pl.when(jnp.logical_and(c != nz - 1, c < last))
+        def _():
+            for k in range(low, high):
+                halo_copy(k).wait_recv()
+
+        @pl.when(c == last)
+        def _():
+            halo_v[0, part] = jnp.zeros(halo_v.shape[2:], BF16)
+
+    @pl.when(c > 0)
+    def _():
+        for k in range(pieces):
+            halo_copy(k).start()
+
+    def tap_copy(chip, slot_at):
+        return pltpu.make_async_remote_copy(
+            src_ref=taps_own, dst_ref=taps_all.at[slot_at], send_sem=tap_send.at[chip],
+            recv_sem=tap_recv.at[slot_at], device_id={"dp": chip * 2 + core}, device_id_type=MESH)
+
+    def own_tap_copy(slot_at):
+        return pltpu.make_async_remote_copy(
+            src_ref=taps_own, dst_ref=taps_all.at[slot_at], send_sem=tap_send.at[d // 2],
+            recv_sem=tap_recv.at[slot_at], device_id=twin, device_id_type=MESH)
+
+    def share_copy(slot_at):
+        return pltpu.make_async_remote_copy(
+            src_ref=taps_all.at[slot_at], dst_ref=taps_all.at[slot_at], send_sem=share_send.at[slot_at // 2],
+            recv_sem=tap_recv.at[slot_at], device_id=twin, device_id_type=MESH)
+
+    def other_chip(k):
+        return (d // 2 + k) % chips
 
     def send_taps(k, carry):
-        tap_copy((d + k) % owners, d).start()
-        return carry
-
-    lax.fori_loop(1, owners, send_taps, 0)
+        tap_copy(other_chip(k), d).start()
+        return carry
+
+    def share_taps(k, carry):
+        p = other_chip(k) * 2 + core
+        tap_copy(other_chip(k), p).wait_recv()
+        share_copy(p).start()
+        return carry
+
+    lax.fori_loop(1, chips, send_taps, 0)
+    own_tap_copy(d).start()
     taps_all[d] = taps_own[...]
 
     def tile_of(ref, index):
@@ -170,10 +242,18 @@
 
         lax.fori_loop(low, high, sixteen, 0)
 
-    def plane_copy(q, slot):
-        return pltpu.make_async_remote_copy(
-            src_ref=send.at[q], dst_ref=recv.at[slot], send_sem=rs_send.at[q],
-            recv_sem=rs_recv.at[slot], device_id=plane_peer(q), device_id_type=MESH)
+    def block_of(owner_core, part, chip):
+        return (owner_core * 2 + part) * chips + chip
+
+    def plane_copy(q, slot_at, part):
+        return pltpu.make_async_remote_copy(
+            src_ref=send.at[block_of(core, part, q // 2)], dst_ref=recv.at[slot_at], send_sem=rs_send.at[q],
+            recv_sem=rs_recv.at[slot_at], device_id=plane_peer(q), device_id_type=MESH)
+
+    def pair_copy(part):
+        return pltpu.make_async_remote_copy(
+            src_ref=send.at[pl.ds(block_of(1 - core, part, 0), chips)], dst_ref=pair.at[part],
+            send_sem=pair_send.at[part], recv_sem=pair_recv.at[part], device_id=twin, device_id_type=MESH)
 
     def out_copy(a):
         rng = pl.ds(pl.multiple_of(a * 16, 16), 16)
@@ -200,53 +280,69 @@
                 obuf[pl.ds(at, 16), j * LANES:(j + 1) * LANES] = jnp.concatenate(v, axis=0).astype(BF16)
         return carry
 
+    lax.fori_loop(0, rows // 16, fill_limits, 0)
     clear(terms)
     cut = rows // 16 - half // 16
     filter_terms(0, cut, 0)
+    lax.fori_loop(1, chips, share_taps, 0)
+    hand_on(0, 2)
     filter_terms(0, cut - half // 16, 1)
+    hand_on(2, 5)
 
     for part in range(2):
-        halos[part].wait_recv()
+        take_halo(part)
 
         def spread_halo(a, carry):
             at = pl.multiple_of(a * 16, 16)
             spread(g_s, rows + part * half + at,
-                   [halo_v[part, pl.ds(at, 16), j * LANES:(j + 1) * LANES].astype(F32) for j in range(tiles)])
+                   [halo_v[slot, part, pl.ds(at, 16), j * LANES:(j + 1) * LANES].astype(F32) for j in range(tiles)])
             return carry
 
         lax.fori_loop(0, half // 16, spread_halo, 0)
         filter_terms(cut - part * (half // 16), rows // 16, part)
-
-        def pack(p, carry):
+        if part == 0:
+            hand_on(5, pieces)
+
+        def pack(chip, carry, owner_core):
             for jj in range(2):
-                tile = p * 2 + jj
+                tile = chip * 4 + owner_core * 2 + jj
                 for tg in range(half // 16):
                     base = ((tile // SUB) * taps + part * half + tg * 16) * SUB + tile % SUB
                     v = [terms[pl.ds(base + h * 8 * SUB, 8, stride=SUB), :] for h in range(2)]
-                    send[p * 2 + part, tg * 16:(tg + 1) * 16, jj * LANES:(jj + 1) * LANES] = (
-                        jnp.concatenate(v, axis=0).astype(BF16))
-            return carry
-
-        lax.fori_loop(0, owners, pack, 0)
-
-        def send_terms(k, carry):
-            q = ((d + k) % owners) * 2 + part
+                    send[block_of(owner_core, part, chip), tg * 16:(tg + 1) * 16,
+                         jj * LANES:(jj + 1) * LANES] = jnp.concatenate(v, axis=0).astype(BF16)
+            return carry
+
+        lax.fori_loop(0, chips, functools.partial(pack, owner_core=1 - core), 0)
+        pair_copy(part).start()
+        lax.fori_loop(0, chips, functools.partial(pack, owner_core=core), 0)
+        pair_copy(part).wait_recv()
+
+        def add_terms(k, carry):
+            chip = other_chip(k)
+            at = block_of(core, part, chip)
+            send[at] = (send[at].astype(F32) + pair[part, chip].astype(F32)).astype(BF16)
+            return carry
+
+        lax.fori_loop(0, chips, add_terms, 0)
+
+        def start_terms(k, carry):
+            q = other_chip(k) * 2 + part
 
             @pl.when(q != me)
             def _():
-                plane_copy(q, me).start()
-
-            return carry
-
-        lax.fori_loop(0, owners, send_terms, 0)
+                plane_copy(q, me, part).start()
+
+            return carry
+
+        lax.fori_loop(0, chips, start_terms, 0)
 
         if part == 0:
             def take_taps(k, carry):
-                p = (d + k) % owners
-                tap_copy(p, p).wait_recv()
+                share_copy(other_chip(k) * 2 + 1 - core).wait_recv()
                 return carry
 
-            lax.fori_loop(1, owners, take_taps, 0)
+            lax.fori_loop(0, chips, take_taps, 0)
 
             def spread_taps(a, carry):
                 at = pl.multiple_of(a * 16, 16)
@@ -257,12 +353,12 @@
             lax.fori_loop(0, taps // 16, spread_taps, 0)
             input_rows(0, 0)
 
-    recv[me] = send[me]
+    recv[me] = send[block_of(core, yh, d // 2)]
     lax.fori_loop(1, 3, input_rows, 0)
 
     def take_terms(k, carry):
         s = (me + k) % group
-        plane_copy(s, s).wait_recv()
+        plane_copy(s, s, yh).wait_recv()
         return carry
 
     lax.fori_loop(1, group, take_terms, 0)
@@ -311,23 +407,36 @@
         return carry
 
     lax.fori_loop(0, rows // 16, end_out, 0)
-    for copy in halos:
-        copy.wait_send()
+    @pl.when(c > 0)
+    def _():
+        for k in range(pieces):
+            halo_copy(k).wait_send()
+
+    @pl.when(hands_on)
+    def _():
+        for k in range(pieces):
+            hand_copy(k).wait_send()
+
     swap_copy(yh).wait_send()
 
     def end_taps(k, carry):
-        tap_copy((d + k) % owners, d).wait_send()
+        tap_copy(other_chip(k), d).wait_send()
+        share_copy(other_chip(k) * 2 + core).wait_send()
         return carry
 
     def end_terms(k, carry):
-        plane_copy((me + k) % group, me).wait_send()
+        q = (me + k) % group
+        plane_copy(q, me, q % 2).wait_send()
         return carry
 
     def end_depth(k, carry):
         depth_copy((z + k) % nz, z).wait_send()
         return carry
 
-    lax.fori_loop(1, owners, end_taps, 0)
+    lax.fori_loop(1, chips, end_taps, 0)
+    own_tap_copy(d).wait_send()
+    for part in range(2):
+        pair_copy(part).wait_send()
     lax.fori_loop(1, group, end_terms, 0)
     lax.fori_loop(1, nz, end_depth, 0)
 
@@ -338,7 +447,6 @@
     half = taps // 2
     owners = lax.axis_size("dp")
     nz = lax.axis_size("ctx") // 2
-    group = 2 * owners
     any_space = pl.BlockSpec(memory_space=pl.ANY)
     vmem = pl.BlockSpec(memory_space=pltpu.VMEM)
     dma = pltpu.SemaphoreType.DMA
@@ -355,7 +463,7 @@
             pltpu.VMEM((rows, channels), BF16),
             pltpu.VMEM((rows, channels), BF16),
             pltpu.VMEM((2, half, channels), BF16),
-            pltpu.VMEM((2, half, channels), BF16),
+            pltpu.VMEM((2, 2, half, channels), BF16),
             pltpu.VMEM(((rows + taps) * SUB, 2 * LANES), BF16),
             pltpu.VMEM((rows * SUB, 2 * LANES), BF16),
             pltpu.VMEM((taps * SUB, 2 * LANES), BF16),
@@ -363,19 +471,25 @@
             pltpu.VMEM((rows, 16 * SUB), F32),
             pltpu.VMEM((2 * taps * SUB, LANES), F32),
             pltpu.VMEM((owners, taps, owned), BF16),
-            pltpu.VMEM((group, half, owned), BF16),
-            pltpu.VMEM((group, half, owned), BF16),
+            pltpu.VMEM((2 * owners, half, owned), BF16),
+            pltpu.VMEM((2, owners // 2, half, owned), BF16),
+            pltpu.VMEM((owners, half, owned), BF16),
             pltpu.VMEM((nz, half, owned), BF16),
             pltpu.VMEM((2, half, owned), F32),
             pltpu.VMEM((2 * ROWS * SUB, LANES), F32),
             pltpu.VMEM((rows, channels), BF16),
             dma((6,)),
+            dma((taps // 8,)),
+            dma((taps // 8,)),
+            dma((taps // 8,)),
+            dma((taps // 8,)),
+            dma((owners // 2,)),
+            dma((owners,)),
+            dma((owners // 2,)),
             dma((2,)),
             dma((2,)),
             dma((owners,)),
             dma((owners,)),
-            dma((group,)),
-            dma((group,)),
             dma((nz,)),
             dma((nz,)),
             dma,

time: 66.9 us -> 66.4 us (level)
  the two profiles are of different devices: /device:TPU:32 before, /device:TPU:6 now
where the time goes in v2:
time: 66.4 us; the launch traced here: 66.2 us
  Pallas kernels  62.6 us (94%)
  local copies, waits for them, and re-layouts  2.95 us (4%)
    pallas_call x1, Pallas kernels, body(): pl.pallas_call(functools.partial(kernel, nz), out_shape=(jax.ShapeDtypeSt...  62.6 us
    unnamed x4, local copies, waits for them, and re-layouts  2.95 us

profile of v2, /device:TPU:6, one launch (start us, length us, event | category | flops | bytes accessed | tf_op | source)
XLA Modules:
  0.0 66.2 jit_solution(4670470256042891240)
XLA Ops:
  0.6 62.6 %conv_backward.1 = (bf16[128,4096]{1,0:T(8,128)(2,1)}, f32[64,256]{1,0:T(8,128)}) custom-call(s32[128]{0:T(128)} %doc_end.1, bf16[128,4096]{1,0:T(8,128)(2,1)} %grad_out.1, bf16[128,4096]{1,0:T(8,128)(2,1)} %gate.1, bf16[128,4096]{1,0:T(8,128)(2,1)} %conv_in.1, bf16[64,256]{1,0:T(8,128)(2,1)} %bitcast.3), custom_call_target="tpu_custom_call" | custom-call | tf_op jit(solution)/shard_map/conv_backward/pallas_call | solution.py:453
  63.2 0.0 copy-start
  63.3 2.3 %copy.9 = bf16[128,4096]{1,0:T(8,128)(2,1)} copy(bf16[128,4096]{1,0:T(8,128)(2,1)} %get-tuple-element.8) | data formatting | bytes 2097152
  65.6 0.0 copy-done
  65.6 0.6 copy.10
Async XLA Ops:
  63.2 2.3 %copy-start = (f32[64,256]{1,0:T(8,128)S(1)}, f32[64,256]{1,0:T(8,128)}, u32[]{:S(2)}) copy-start(f32[64,256]{1,0:T(8,128)} %get-tuple-element.5) | copy-start | bytes 196612

commit v3 on v2

--- a/solution.py
+++ b/solution.py
@@ -259,6 +259,13 @@
         rng = pl.ds(pl.multiple_of(a * 16, 16), 16)
         return pltpu.make_async_copy(obuf.at[rng], grad_in.at[rng], out_sem.at[a])
 
+    def out_rows(low, high):
+        def start_out(a, carry):
+            out_copy(a).start()
+            return carry
+
+        lax.fori_loop(low * (ROWS // 16), high * (ROWS // 16), start_out, 0)
+
     def input_rows(chunk, carry):
         clear(o32)
 
@@ -337,24 +344,21 @@
 
         lax.fori_loop(0, chips, start_terms, 0)
 
-        if part == 0:
-            def take_taps(k, carry):
-                share_copy(other_chip(k) * 2 + 1 - core).wait_recv()
-                return carry
-
-            lax.fori_loop(0, chips, take_taps, 0)
-
-            def spread_taps(a, carry):
-                at = pl.multiple_of(a * 16, 16)
-                spread(f_s, at, [taps_all[j // 2, pl.ds(at, 16), (j % 2) * LANES:(j % 2 + 1) * LANES].astype(F32)
-                                 for j in range(tiles)])
-                return carry
-
-            lax.fori_loop(0, taps // 16, spread_taps, 0)
-            input_rows(0, 0)
-
     recv[me] = send[block_of(core, yh, d // 2)]
-    lax.fori_loop(1, 3, input_rows, 0)
+    def take_taps(k, carry):
+        share_copy(other_chip(k) * 2 + 1 - core).wait_recv()
+        return carry
+
+    lax.fori_loop(0, chips, take_taps, 0)
+
+    def spread_taps(a, carry):
+        at = pl.multiple_of(a * 16, 16)
+        spread(f_s, at, [taps_all[j // 2, pl.ds(at, 16), (j % 2) * LANES:(j % 2 + 1) * LANES].astype(F32)
+                         for j in range(tiles)])
+        return carry
+
+    lax.fori_loop(0, taps // 16, spread_taps, 0)
+    input_rows(0, 0)
 
     def take_terms(k, carry):
         s = (me + k) % group
@@ -376,7 +380,8 @@
         return carry
 
     lax.fori_loop(1, nz, send_depth, 0)
-    lax.fori_loop(3, rows // ROWS, input_rows, 0)
+    lax.fori_loop(1, 3, input_rows, 0)
+    out_rows(0, 2)
 
     def take_depth(k, carry):
         other = (z + k) % nz
@@ -392,12 +397,8 @@
             device_id={"ctx": (1 - yh) * nz + z}, device_id_type=MESH)
 
     swap_copy(yh).start()
-
-    def start_out(a, carry):
-        out_copy(a).start()
-        return carry
-
-    lax.fori_loop(0, rows // 16, start_out, 0)
+    lax.fori_loop(3, rows // ROWS, input_rows, 0)
+    out_rows(2, rows // ROWS)
     swap_copy(1 - yh).wait_recv()
     grad_filt[0:half, :] = ybuf[0]
     grad_filt[half:taps, :] = ybuf[1]

time: 66.4 us -> 63.1 us (0.950)
  the two profiles are of different devices: /device:TPU:6 before, /device:TPU:1 now
where the time goes in v3:
time: 63.1 us; the launch traced here: 62.9 us
  Pallas kernels  59.3 us (94%)
  local copies, waits for them, and re-layouts  2.95 us (5%)
  between operations  0.65 us (1%)
    pallas_call x1, Pallas kernels, body(): pl.pallas_call(functools.partial(kernel, nz), out_shape=(jax.ShapeDtypeSt...  59.3 us
    unnamed x4, local copies, waits for them, and re-layouts  2.95 us

profile of v3, /device:TPU:1, one launch (start us, length us, event | category | flops | bytes accessed | tf_op | source)
XLA Modules:
  0.0 62.9 jit_solution(16126201646232719288)
XLA Ops:
  0.6 59.3 %conv_backward.1 = (bf16[128,4096]{1,0:T(8,128)(2,1)}, f32[64,256]{1,0:T(8,128)}) custom-call(s32[128]{0:T(128)} %doc_end.1, bf16[128,4096]{1,0:T(8,128)(2,1)} %grad_out.1, bf16[128,4096]{1,0:T(8,128)(2,1)} %gate.1, bf16[128,4096]{1,0:T(8,128)(2,1)} %conv_in.1, bf16[64,256]{1,0:T(8,128)(2,1)} %bitcast.3), custom_call_target="tpu_custom_call" | custom-call | tf_op jit(solution)/shard_map/conv_backward/pallas_call | solution.py:454
  59.9 0.0 copy-start
  59.9 2.3 %copy.9 = bf16[128,4096]{1,0:T(8,128)(2,1)} copy(bf16[128,4096]{1,0:T(8,128)(2,1)} %get-tuple-element.8) | data formatting | bytes 2097152
  62.2 0.0 copy-done
  62.2 0.6 %copy.10 = f32[256,64]{0,1:T(8,128)} copy(f32[256,64]{0,1:T(8,128)S(1)} %bitcast.2) | data formatting | bytes 131072
Async XLA Ops:
  59.9 2.3 %copy-start = (f32[64,256]{1,0:T(8,128)S(1)}, f32[64,256]{1,0:T(8,128)}, u32[]{:S(2)}) copy-start(f32[64,256]{1,0:T(8,128)} %get-tuple-element.5) | copy-start | bytes 196612

commit v4 on v3

--- a/solution.py
+++ b/solution.py
@@ -296,6 +296,28 @@
     filter_terms(0, cut - half // 16, 1)
     hand_on(2, 5)
 
+    def finish(part):
+        pair_copy(part).wait_recv()
+
+        def add_terms(k, carry):
+            chip = other_chip(k)
+            at = block_of(core, part, chip)
+            send[at] = (send[at].astype(F32) + pair[part, chip].astype(F32)).astype(BF16)
+            return carry
+
+        lax.fori_loop(0, chips, add_terms, 0)
+
+        def start_terms(k, carry):
+            q = other_chip(k) * 2 + part
+
+            @pl.when(q != me)
+            def _():
+                plane_copy(q, me, part).start()
+
+            return carry
+
+        lax.fori_loop(0, chips, start_terms, 0)
+
     for part in range(2):
         take_halo(part)
 
@@ -306,7 +328,10 @@
             return carry
 
         lax.fori_loop(0, half // 16, spread_halo, 0)
-        filter_terms(cut - part * (half // 16), rows // 16, part)
+        if part == 1:
+            filter_terms(cut - half // 16, cut, part)
+            finish(0)
+        filter_terms(cut, rows // 16, part)
         if part == 0:
             hand_on(5, pieces)
 
@@ -323,28 +348,7 @@
         lax.fori_loop(0, chips, functools.partial(pack, owner_core=1 - core), 0)
         pair_copy(part).start()
         lax.fori_loop(0, chips, functools.partial(pack, owner_core=core), 0)
-        pair_copy(part).wait_recv()
-
-        def add_terms(k, carry):
-            chip = other_chip(k)
-            at = block_of(core, part, chip)
-            send[at] = (send[at].astype(F32) + pair[part, chip].astype(F32)).astype(BF16)
-            return carry
-
-        lax.fori_loop(0, chips, add_terms, 0)
-
-        def start_terms(k, carry):
-            q = other_chip(k) * 2 + part
-
-            @pl.when(q != me)
-            def _():
-                plane_copy(q, me, part).start()
-
-            return carry
-
-        lax.fori_loop(0, chips, start_terms, 0)
-
-    recv[me] = send[block_of(core, yh, d // 2)]
+
     def take_taps(k, carry):
         share_copy(other_chip(k) * 2 + 1 - core).wait_recv()
         return carry
@@ -358,6 +362,8 @@
         return carry
 
     lax.fori_loop(0, taps // 16, spread_taps, 0)
+    finish(1)
+    recv[me] = send[block_of(core, yh, d // 2)]
     input_rows(0, 0)
 
     def take_terms(k, carry):

time: 63.1 us -> 63.1 us (level)
  the two profiles are of different devices: /device:TPU:1 before, /device:TPU:6 now
where the time goes in v4:
time: 63.1 us; the launch traced here: 61.9 us
  Pallas kernels  58.3 us (92%)
  local copies, waits for them, and re-layouts  2.95 us (5%)
  between operations  0.65 us (1%)
    pallas_call x1, Pallas kernels, body(): pl.pallas_call(functools.partial(kernel, nz), out_shape=(jax.ShapeDtypeSt...  58.3 us
    unnamed x4, local copies, waits for them, and re-layouts  2.95 us

profile of v4, /device:TPU:6, one launch (start us, length us, event | category | flops | bytes accessed | tf_op | source)
XLA Modules:
  0.0 61.9 jit_solution(12556171295164008101)
XLA Ops:
  0.6 58.3 %conv_backward.1 = (bf16[128,4096]{1,0:T(8,128)(2,1)}, f32[64,256]{1,0:T(8,128)}) custom-call(s32[128]{0:T(128)} %doc_end.1, bf16[128,4096]{1,0:T(8,128)(2,1)} %grad_out.1, bf16[128,4096]{1,0:T(8,128)(2,1)} %gate.1, bf16[128,4096]{1,0:T(8,128)(2,1)} %conv_in.1, bf16[64,256]{1,0:T(8,128)(2,1)} %bitcast.3), custom_call_target="tpu_custom_call" | custom-call | tf_op jit(solution)/shard_map/conv_backward/pallas_call | solution.py:460
  58.9 0.0 copy-start
  58.9 2.3 %copy.9 = bf16[128,4096]{1,0:T(8,128)(2,1)} copy(bf16[128,4096]{1,0:T(8,128)(2,1)} %get-tuple-element.8) | data formatting | bytes 2097152
  61.3 0.0 copy-done
  61.3 0.6 %copy.10 = f32[256,64]{0,1:T(8,128)} copy(f32[256,64]{0,1:T(8,128)S(1)} %bitcast.2) | data formatting | bytes 131072
Async XLA Ops:
  58.9 2.3 %copy-start = (f32[64,256]{1,0:T(8,128)S(1)}, f32[64,256]{1,0:T(8,128)}, u32[]{:S(2)}) copy-start(f32[64,256]{1,0:T(8,128)} %get-tuple-element.5) | copy-start | bytes 196612
